TPU v7x, 32 devices: a whole 2x2x4 slice. The times are simulated.
32 devices in a mesh: patch: 8 (over z, x), rep: 4 (over y, core).
Axes of the slice: x: 2, y: 2, z: 4, core: 2. Of those that a mesh axis runs over, the one named last changes fastest.
Arguments:
- node_latents: bfloat16 [4, 3072, 512], P('rep', 'patch'), may hold values from -6 to 6
- edge_latents: bfloat16 [4, 10240, 512], P('rep', 'patch'), may hold values from -6 to 6
- targets: bfloat16 [4, 3072, 128], P('rep', 'patch'), may hold values from -6 to 6
- edge_weight_in: bfloat16 [1536, 512], replicated, may hold values from -0.15625 to 0.15625
- edge_weight_out: bfloat16 [512, 512], replicated, may hold values from -0.25 to 0.25
- node_weight_in: bfloat16 [1024, 512], replicated, may hold values from -0.1875 to 0.1875
- node_weight_out: bfloat16 [512, 512], replicated, may hold values from -0.25 to 0.25
- readout_weight: bfloat16 [512, 128], replicated, may hold values from -0.25 to 0.25
- send_rows: int32 [8, 96], P('patch'), may hold values from 0 to 383, as said below
- far_rows: int32 [8, 8], P('patch'), may hold values from 0 to 383, as said below
- edge_sender: int32 [10240], P('patch'), may hold values from 0 to 487
- edge_receiver: int32 [10240], P('patch'), may hold values from 0 to 383
- edge_count: int32 [8], P('patch'), may hold values from 80 to 1280, as said below
- land_mask: int32 [3072], P('patch'), may hold values 0 or 1
- lat_band: int32 [3072], P('patch'), may hold values from 0 to 720
Outputs:
- node_grad: bfloat16 [4, 3072, 512], P('rep', 'patch')
- edge_grad: bfloat16 [4, 10240, 512], P('rep', 'patch')
- grad_edge_in: float32 [1536, 512], P('patch')
- grad_edge_out: float32 [512, 512], P('patch')
- grad_node_in: float32 [1024, 512], P('patch')
- grad_node_out: float32 [512, 512], P('patch')
- grad_readout: float32 [512, 128], P('patch')
Inputs may be any that keep to these rules, and one draw needn't show every extreme that they name: `send_rows`: the 16 entries of a patch for one neighbour are distinct. `far_rows`: each patch sends exactly one node to every patch (itself included). `edge_count`: some patch has all 1280 edges live.
All inputs are finite; a program needn't handle non-finite values. No bound on the sum of `land_mask` on one device may be relied on, other than what follows from the above.
Results may differ from a plain program's by a relative error of at most 0.012.
Values may be sent and summed in bfloat16 or wider, within the bound.
A program may use at most 128 MiB of HBM per device.

v0:
```python
import jax
import jax.numpy as jnp
from jax import lax
from jax.sharding import PartitionSpec as P

OCEAN = 32
BANDS = 721


def passed_along(x, axis, by):
    peers = lax.axis_size(axis)
    return lax.ppermute(x, axis, [(i, (i + by) % peers) for i in range(peers)])


def normalize(values):
    average = jnp.mean(values, axis=-1, keepdims=True)
    centred = values - average
    variance = jnp.mean(centred * centred, axis=-1, keepdims=True)
    inverse = lax.rsqrt(variance + 1e-05)
    return (centred * inverse, inverse)


def norm_back(gradient, normed, inverse):
    first = jnp.mean(gradient, axis=-1, keepdims=True)
    second = jnp.mean(gradient * normed, axis=-1, keepdims=True)
    return inverse * (gradient - first - normed * second)


def silu_grad(values):
    logistic = jax.nn.sigmoid(values)
    return logistic * (1.0 + values * (1.0 - logistic))


def product(left, right):
    return jnp.dot(left, right, preferred_element_type=jnp.float32)


def product_left(left, right):
    return lax.dot_general(
        left, right, (((0,), (0,)), ((), ())), preferred_element_type=jnp.float32
    )


def product_right(left, right):
    return lax.dot_general(
        left, right, (((1,), (1,)), ((), ())), preferred_element_type=jnp.float32
    )


def body(
    node_latents,
    edge_latents,
    targets,
    edge_weight_in,
    edge_weight_out,
    node_weight_in,
    node_weight_out,
    readout_weight,
    send_rows,
    far_rows,
    edge_sender,
    edge_receiver,
    edge_count,
    land_mask,
    lat_band,
):
    model_width = node_latents.shape[2]
    local_nodes = node_latents.shape[1]
    local_edges = edge_latents.shape[1]
    patches = lax.axis_size("patch")
    replicas = lax.axis_size("rep")
    offsets = (1, -1, 2, -2, 3, -3)
    near_width = send_rows.shape[1] // 6
    near_total = local_nodes + 6 * near_width
    node_rows = node_latents[0]
    edge_rows = edge_latents[0]
    target = targets[0].astype(jnp.float32)
    outgoing = node_rows[send_rows[0]]
    near_blocks = []
    for neighbour, offset in enumerate(offsets):
        piece = outgoing[neighbour * near_width : (neighbour + 1) * near_width]
        near_blocks.append(passed_along(piece, "patch", offset))
    far_incoming = lax.all_to_all(
        node_rows[far_rows[0]], "patch", split_axis=0, concat_axis=0, tiled=True
    )
    extended = jnp.concatenate([node_rows] + near_blocks + [far_incoming], axis=0)
    sender_rows = extended[edge_sender]
    receiver_rows = node_rows[edge_receiver]
    positions = lax.iota(jnp.int32, local_edges)
    alive_mask = (positions < edge_count[0]).astype(jnp.float32)[:, None]
    stacked = jnp.concatenate([sender_rows, receiver_rows, edge_rows], axis=1)
    edge_pre = product(stacked, edge_weight_in)
    edge_hidden = jax.nn.silu(edge_pre).astype(jnp.bfloat16)
    edge_normed, edge_inverse = normalize(product(edge_hidden, edge_weight_out))
    message = (edge_normed * alive_mask).astype(jnp.bfloat16)
    node_ids = lax.iota(jnp.int32, local_nodes)
    receiver_table = (edge_receiver[:, None] == node_ids[None, :]).astype(jnp.bfloat16)
    aggregate = product_left(receiver_table, message).astype(jnp.bfloat16)
    node_input = jnp.concatenate([node_rows, aggregate], axis=1)
    node_pre = product(node_input, node_weight_in)
    node_hidden = jax.nn.silu(node_pre).astype(jnp.bfloat16)
    node_normed, node_inverse = normalize(product(node_hidden, node_weight_out))
    updated = (node_rows.astype(jnp.float32) + node_normed).astype(jnp.bfloat16)
    predicted = product(updated, readout_weight)
    latitude = -0.5 * jnp.pi + (lat_band.astype(jnp.float32) + 0.5) * (jnp.pi / BANDS)
    channel = lax.iota(jnp.int32, readout_weight.shape[1])
    keep_mask = jnp.where((channel[None, :] < OCEAN) & (land_mask[:, None] == 1), 0.0, 1.0)
    loss_weight = jnp.cos(latitude)[:, None] * keep_mask
    pred_grad = (loss_weight * (predicted - target)).astype(jnp.bfloat16)
    updated_grad = product_right(pred_grad, readout_weight)
    node_z_grad = norm_back(updated_grad, node_normed, node_inverse).astype(jnp.bfloat16)
    node_pre_grad = (product_right(node_z_grad, node_weight_out) * silu_grad(node_pre)).astype(
        jnp.bfloat16
    )
    input_grad = product_right(node_pre_grad, node_weight_in)
    message_grad = input_grad[:, model_width:][edge_receiver] * alive_mask
    edge_z_grad = norm_back(message_grad, edge_normed, edge_inverse).astype(jnp.bfloat16)
    edge_pre_grad = (product_right(edge_z_grad, edge_weight_out) * silu_grad(edge_pre)).astype(
        jnp.bfloat16
    )
    stacked_grad = product_right(edge_pre_grad, edge_weight_in)
    sender_grad = stacked_grad[:, :model_width].astype(jnp.bfloat16)
    receiver_grad = stacked_grad[:, model_width : 2 * model_width].astype(jnp.bfloat16)
    edge_result = stacked_grad[:, 2 * model_width :].astype(jnp.bfloat16)
    extended_ids = lax.iota(jnp.int32, extended.shape[0])
    sender_table = (edge_sender[:, None] == extended_ids[None, :]).astype(jnp.bfloat16)
    extended_grad = product_left(sender_table, sender_grad)
    back_blocks = []
    for neighbour, offset in enumerate(offsets):
        block = extended_grad[
            local_nodes + neighbour * near_width : local_nodes + (neighbour + 1) * near_width
        ]
        back_blocks.append(
            passed_along(block.astype(jnp.bfloat16), "patch", -offset).astype(block.dtype)
        )
    far_returned = lax.all_to_all(
        extended_grad[near_total:].astype(jnp.bfloat16),
        "patch",
        split_axis=0,
        concat_axis=0,
        tiled=True,
    ).astype(jnp.float32)
    returned = jnp.concatenate(back_blocks + [far_returned], axis=0)
    owners = jnp.concatenate([send_rows[0], far_rows[0]], axis=0)
    return_table = (owners[:, None] == node_ids[None, :]).astype(jnp.float32)
    owned_grad = lax.dot_general(
        return_table,
        returned,
        (((0,), (0,)), ((), ())),
        precision=lax.Precision.HIGHEST,
        preferred_element_type=jnp.float32,
    )
    total = updated_grad + input_grad[:, :model_width] + extended_grad[:local_nodes]
    total = total + product_left(receiver_table, receiver_grad) + owned_grad
    grad_scale = 1.0 / (local_nodes * patches * replicas)
    weight_grads = (
        product_left(stacked, edge_pre_grad) * grad_scale,
        product_left(edge_hidden, edge_z_grad) * grad_scale,
        product_left(node_input, node_pre_grad) * grad_scale,
        product_left(node_hidden, node_z_grad) * grad_scale,
        product_left(updated, pred_grad) * grad_scale,
    )
    pieces = tuple((gradient.reshape(patches * replicas, -1) for gradient in weight_grads))
    shares = lax.psum_scatter(pieces, ("patch", "rep"), scatter_dimension=0, tiled=True)
    regrouped = lax.all_gather(shares, "rep", axis=1, tiled=True)
    reduced = tuple(
        (
            joined.reshape(gradient.shape[0] // patches, gradient.shape[1])
            for joined, gradient in zip(regrouped, weight_grads)
        )
    )
    return (
        total.astype(jnp.bfloat16)[None],
        edge_result[None],
        reduced[0],
        reduced[1],
        reduced[2],
        reduced[3],
        reduced[4],
    )


def solution(mesh):
    in_specs = (
        P("rep", "patch", None),
        P("rep", "patch", None),
        P("rep", "patch", None),
        P(),
        P(),
        P(),
        P(),
        P(),
        P("patch", None),
        P("patch", None),
        P("patch"),
        P("patch"),
        P("patch"),
        P("patch"),
        P("patch"),
    )
    out_specs = (
        P("rep", "patch", None),
        P("rep", "patch", None),
        P("patch", None),
        P("patch", None),
        P("patch", None),
        P("patch", None),
        P("patch", None),
    )
    return jax.shard_map(body, mesh=mesh, in_specs=in_specs, out_specs=out_specs, check_vma=False)
```

profile of v0, /device:TPU:0, one launch (start us, length us, event | category | flops | bytes accessed | tf_op | source)
XLA Modules:
  0.0 323.7 jit_solution(2228589647517178149)
XLA Ops:
  10.5 3.0 collective-permute-start
  13.5 3.1 collective-permute-start.1
  16.6 3.8 %collective-permute-start.3 = (bf16[16,512]{1,0:T(8,128)(2,1)S(1)}, bf16[16,512]{1,0:T(8,128)(2,1)S(1)}, u32[]{:S(2)}, u32[]{:S(2)}) collective-permute-start(bf16[16,512]{1,0:T(8,128)(2,1)S(1)} %get-tuple-element.24), channel_id=1, source_target_pairs={{0,24},{4,28},{8,0},{12,4},{16,8},{20,12},{24,16},{28,20},{1,25},{... | collective-permute-start | bytes 49160 | tf_op jit(solution)/shard_map/ppermute | solution.py:12
  23.9 5.1 %all-to-all-start = ((bf16[8,2,256]{2,1,0:T(2,128)(2,1)}), bf16[8,2,256]{2,1,0:T(2,128)(2,1)S(1)}, u32[]{:S(2)}, u32[]{:S(2)}) async-start(bf16[8,2,256]{2,1,0:T(2,128)(2,1)} %reshape.248), calls=%async_computation | async-start | bytes 16384 | tf_op jit(solution)/shard_map/all_to_all | solution.py:83
  33.6 4.7 %gather_fusion.3 = bf16[1280,512]{1,0:T(8,128)(2,1)} fusion(bf16[384,512]{1,0:T(8,128)(2,1)S(1)} %bitcast.58, s32[2048]{0:T(1024)S(1)} %get-tuple-element.37), kind=kCustom, calls=%fused_computation.3 | custom fusion | bytes 2626560 | tf_op jit(solution)/shard_map/gather | solution.py:88
  38.3 3.8 %collective-permute-start.5 = (bf16[16,512]{1,0:T(8,128)(2,1)S(1)}, bf16[16,512]{1,0:T(8,128)(2,1)S(1)}, u32[]{:S(2)}, u32[]{:S(2)}) collective-permute-start(bf16[16,512]{1,0:T(8,128)(2,1)S(1)} %get-tuple-element.22), channel_id=1, source_target_pairs={{0,20},{4,24},{8,28},{12,0},{16,4},{20,8},{24,12},{28,16},{1,21},{... | collective-permute-start | bytes 49160 | tf_op jit(solution)/shard_map/ppermute | solution.py:12
  43.6 4.7 %gather_fusion.2 = bf16[1280,512]{1,0:T(8,128)(2,1)} fusion(bf16[488,512]{1,0:T(8,128)(2,1)S(1)} %constant_dynamic-update-slice_fusion, s32[2048]{0:T(1024)S(1)} %get-tuple-element.38), kind=kCustom, calls=%fused_computation.2 | custom fusion | bytes 2626560 | tf_op jit(solution)/shard_map/gather | solution.py:87
  48.3 6.1 %multiply_convert_fusion.2 = (bf16[1280,512]{1,0:T(8,128)(2,1)S(1)}, f32[1280,512]{1,0:T(8,128)}) fusion(bf16[1536,512]{1,0:T(8,128)(2,1)S(1)} %copy-done, bf16[1280,512]{1,0:T(8,128)(2,1)} %bitcast.63, bf16[1280,512]{1,0:T(8,128)(2,1)} %gather_fusion.3, bf16[1280,512]{1,0:T(8,128)(2,1)} %gather_fusion.2), kind=kOutput, calls=%fused_computation.15 | convolution fusion | flops 2028339200 | bytes 9437184 | tf_op jit(solution)/shard_map/dot_general | solution.py:35
  66.3 4.5 %gather_fusion.4 = f32[1280,512]{1,0:T(8,128)} fusion(f32[384,512]{1,0:T(8,128)S(1)} %slice.103, s32[2048]{0:T(1024)S(1)} %get-tuple-element.37), kind=kCustom, calls=%fused_computation.4 | custom fusion | bytes 5248000 | tf_op jit(solution)/shard_map/gather | solution.py:116
  70.8 3.2 copy.27
  74.0 3.2 multiply_reduce_fusion.2
  83.9 3.7 %convolution_multiply_fusion.1 = f32[1536,512]{1,0:T(8,128)} fusion(bf16[1280,512]{1,0:T(8,128)(2,1)S(1)} %fusion, bf16[1280,512]{1,0:T(8,128)(2,1)S(1)} %bitcast.64, bf16[1280,512]{1,0:T(8,128)(2,1)S(1)} %copy-done.9, bf16[1280,512]{1,0:T(8,128)(2,1)S(1)} %copy-done.10), kind=kOutput, calls=%fused_computation.8 | convolution fusion | flops 2025848832 | bytes 8388608 | tf_op jit(solution)/shard_map/dot_general | solution.py:39
  87.6 3.4 %reshape.164 = f32[32,24576]{1,0:T(8,128)} reshape(f32[1536,512]{1,0:T(8,128)} %convolution_multiply_fusion.1) | data formatting | bytes 6291456 | tf_op jit(solution)/shard_map/reshape | solution.py:163
  107.0 5.2 %collective-permute-start.6 = (bf16[16,512]{1,0:T(8,128)(2,1)S(1)}, bf16[16,512]{1,0:T(8,128)(2,1)S(1)}, u32[]{:S(2)}, u32[]{:S(2)}) collective-permute-start(bf16[16,512]{1,0:T(8,128)(2,1)S(1)} %get-tuple-element.21), channel_id=1, source_target_pairs={{0,28},{4,0},{8,4},{12,8},{16,12},{20,16},{24,20},{28,24},{1,29},{... | collective-permute-start | bytes 49160 | tf_op jit(solution)/shard_map/ppermute | solution.py:12
  114.3 3.3 %collective-permute-start.10 = (bf16[16,512]{1,0:T(8,128)(2,1)S(1)}, bf16[16,512]{1,0:T(8,128)(2,1)S(1)}, u32[]{:S(2)}, u32[]{:S(2)}) collective-permute-start(bf16[16,512]{1,0:T(8,128)(2,1)S(1)} %get-tuple-element.17), channel_id=1, source_target_pairs={{0,20},{4,24},{8,28},{12,0},{16,4},{20,8},{24,12},{28,16},{1,21},{... | collective-permute-start | bytes 49160 | tf_op jit(solution)/shard_map/ppermute | solution.py:12
  118.8 5.1 %all-to-all-start.1 = ((bf16[8,2,256]{2,1,0:T(2,128)(2,1)}), bf16[8,2,256]{2,1,0:T(2,128)(2,1)S(1)}, u32[]{:S(2)}, u32[]{:S(2)}) async-start(bf16[8,2,256]{2,1,0:T(2,128)(2,1)} %reshape.250), calls=%async_computation.1 | async-start | bytes 16384 | tf_op jit(solution)/shard_map/all_to_all | solution.py:136
  126.6 3.4 %fusion.12 = f32[384,512]{1,0:T(8,128)} fusion(bf16[1280,1536]{1,0:T(8,128)(2,1)} %copy-done.15, s32[1280]{0:T(1024)S(1)} %copy-done.18, f32[488,512]{1,0:T(8,128)S(1)} %copy-done.24, f32[384,512]{1,0:T(8,128)S(1)} %copy-done.8, f32[384,1024]{1,0:T(8,128)S(1)} %copy-done.6), kind=kOutput, calls=%fused_computation.37 | convolution fusion | flops 504397824 | bytes 4461568 | tf_op jit(solution)/shard_map/dot_general | solution.py:39
  133.1 3.7 %collective-permute-done.11 = bf16[16,512]{1,0:T(8,128)(2,1)S(1)} collective-permute-done((bf16[16,512]{1,0:T(8,128)(2,1)S(1)}, bf16[16,512]{1,0:T(8,128)(2,1)S(1)}, u32[]{:S(2)}, u32[]{:S(2)}) %collective-permute-start.11) | collective-permute-done | bytes 16416 | tf_op jit(solution)/shard_map/ppermute | solution.py:12
  139.1 135.3 %all-reduce.8.cloned.1.call-done = (f32[32,24576]{1,0:T(8,128)}, f32[32,8192]{1,0:T(8,128)}, f32[32,16384]{1,0:T(8,128)}, f32[32,8192]{1,0:T(8,128)}, f32[32,2048]{1,0:T(8,128)}) async-done(((f32[32,24576]{1,0:T(8,128)}, f32[32,8192]{1,0:T(8,128)}, f32[32,16384]{1,0:T(8,128)}, f32[32,8192]{1,0:T(8,128)}, f32[32,2048]{1,0:T(8,128)}), (f32[32,24576]{1,0:T(8,128)}, f32[32,8192]{1,0:T(8,128)}, ...) | async-done | bytes 7602192
  275.6 6.7 %all_gather.15 = f32[1,98304]{1,0:T(1,128)S(1)} all-gather(f32[1,24576]{1,0:T(1,128)S(1)} %constant_dynamic-slice_fusion.4), channel_id=1, replica_groups=mesh['patch'=8,'rep'=4] {'rep'}, dimensions={1}, use_global_device_ids=true | all-gather | bytes 491520 | tf_op jit(solution)/shard_map/all_gather | solution.py:165
  286.2 5.9 %all_gather.17 = f32[1,65536]{1,0:T(1,128)S(1)} all-gather(f32[1,16384]{1,0:T(1,128)S(1)} %constant_dynamic-slice_fusion.2), channel_id=1, replica_groups=mesh['patch'=8,'rep'=4] {'rep'}, dimensions={1}, use_global_device_ids=true | all-gather | bytes 327680 | tf_op jit(solution)/shard_map/all_gather | solution.py:165
  295.1 5.4 %all_gather.16 = f32[1,32768]{1,0:T(1,128)S(1)} all-gather(f32[1,8192]{1,0:T(1,128)S(1)} %constant_dynamic-slice_fusion.3), channel_id=1, replica_groups=mesh['patch'=8,'rep'=4] {'rep'}, dimensions={1}, use_global_device_ids=true | all-gather | bytes 163840 | tf_op jit(solution)/shard_map/all_gather | solution.py:165
  303.1 5.4 %all_gather.18 = f32[1,32768]{1,0:T(1,128)S(1)} all-gather(f32[1,8192]{1,0:T(1,128)S(1)} %constant_dynamic-slice_fusion.1), channel_id=1, replica_groups=mesh['patch'=8,'rep'=4] {'rep'}, dimensions={1}, use_global_device_ids=true | all-gather | bytes 163840 | tf_op jit(solution)/shard_map/all_gather | solution.py:165
  311.0 5.2 %all_gather.19 = f32[1,8192]{1,0:T(1,128)S(1)} all-gather(f32[1,2048]{1,0:T(1,128)S(1)} %constant_dynamic-slice_fusion), channel_id=1, replica_groups=mesh['patch'=8,'rep'=4] {'rep'}, dimensions={1}, use_global_device_ids=true | all-gather | bytes 40960 | tf_op jit(solution)/shard_map/all_gather | solution.py:165
  (165 shorter events, 71.4 us)
Async XLA Ops:
  7.2 41.1 %copy-start = (bf16[1536,512]{1,0:T(8,128)(2,1)S(1)}, bf16[1536,512]{1,0:T(8,128)(2,1)}, u32[]{:S(2)}) copy-start(bf16[1536,512]{1,0:T(8,128)(2,1)} %param.18) | copy-start | bytes 4718596
  7.2 26.4 %copy-start.1 = (bf16[1,384,512]{2,1,0:T(8,128)(2,1)S(1)}, bf16[1,384,512]{2,1,0:T(8,128)(2,1)}, u32[]{:S(2)}) copy-start(bf16[1,384,512]{2,1,0:T(8,128)(2,1)} %param.15) | copy-start | bytes 1179652
  10.5 27.8 %collective-permute-start = (bf16[16,512]{1,0:T(8,128)(2,1)S(1)}, bf16[16,512]{1,0:T(8,128)(2,1)S(1)}, u32[]{:S(2)}, u32[]{:S(2)}) collective-permute-start(bf16[16,512]{1,0:T(8,128)(2,1)S(1)} %get-tuple-element.27), channel_id=1, source_target_pairs={{0,4},{4,8},{8,12},{12,16},{16,20},{20,24},{24,28},{28,0},{1,5},{5... | collective-permute-start | bytes 49160 | tf_op jit(solution)/shard_map/ppermute | solution.py:12
  13.5 28.6 %collective-permute-start.1 = (bf16[16,512]{1,0:T(8,128)(2,1)S(1)}, bf16[16,512]{1,0:T(8,128)(2,1)S(1)}, u32[]{:S(2)}, u32[]{:S(2)}) collective-permute-start(bf16[16,512]{1,0:T(8,128)(2,1)S(1)} %get-tuple-element.26), channel_id=1, source_target_pairs={{0,28},{4,0},{8,4},{12,8},{16,12},{20,16},{24,20},{28,24},{1,29},{... | collective-permute-start | bytes 49160 | tf_op jit(solution)/shard_map/ppermute | solution.py:12
  16.6 25.5 %collective-permute-start.2 = (bf16[16,512]{1,0:T(8,128)(2,1)S(1)}, bf16[16,512]{1,0:T(8,128)(2,1)S(1)}, u32[]{:S(2)}, u32[]{:S(2)}) collective-permute-start(bf16[16,512]{1,0:T(8,128)(2,1)S(1)} %get-tuple-element.25), channel_id=1, source_target_pairs={{0,8},{4,12},{8,16},{12,20},{16,24},{20,28},{24,0},{28,4},{1,9},{5... | collective-permute-start | bytes 49160 | tf_op jit(solution)/shard_map/ppermute | solution.py:12
  16.6 25.5 %collective-permute-start.3 = (bf16[16,512]{1,0:T(8,128)(2,1)S(1)}, bf16[16,512]{1,0:T(8,128)(2,1)S(1)}, u32[]{:S(2)}, u32[]{:S(2)}) collective-permute-start(bf16[16,512]{1,0:T(8,128)(2,1)S(1)} %get-tuple-element.24), channel_id=1, source_target_pairs={{0,24},{4,28},{8,0},{12,4},{16,8},{20,12},{24,16},{28,20},{1,25},{... | collective-permute-start | bytes 49160 | tf_op jit(solution)/shard_map/ppermute | solution.py:12
  20.5 21.7 %collective-permute-start.4 = (bf16[16,512]{1,0:T(8,128)(2,1)S(1)}, bf16[16,512]{1,0:T(8,128)(2,1)S(1)}, u32[]{:S(2)}, u32[]{:S(2)}) collective-permute-start(bf16[16,512]{1,0:T(8,128)(2,1)S(1)} %get-tuple-element.23), channel_id=1, source_target_pairs={{0,12},{4,16},{8,20},{12,24},{16,28},{20,0},{24,4},{28,8},{1,13},{... | collective-permute-start | bytes 49160 | tf_op jit(solution)/shard_map/ppermute | solution.py:12
  23.9 14.4 %all-to-all-start = ((bf16[8,2,256]{2,1,0:T(2,128)(2,1)}), bf16[8,2,256]{2,1,0:T(2,128)(2,1)S(1)}, u32[]{:S(2)}, u32[]{:S(2)}) async-start(bf16[8,2,256]{2,1,0:T(2,128)(2,1)} %reshape.248), calls=%async_computation | async-start | bytes 16384 | tf_op jit(solution)/shard_map/all_to_all | solution.py:83
  29.0 245.4 %all-reduce.8.cloned.1.call-start = ((), (), s32[]{:S(2)}) async-start(), calls=%async_computation.2 | async-start | bytes 15204352
  38.3 5.3 %collective-permute-start.5 = (bf16[16,512]{1,0:T(8,128)(2,1)S(1)}, bf16[16,512]{1,0:T(8,128)(2,1)S(1)}, u32[]{:S(2)}, u32[]{:S(2)}) collective-permute-start(bf16[16,512]{1,0:T(8,128)(2,1)S(1)} %get-tuple-element.22), channel_id=1, source_target_pairs={{0,20},{4,24},{8,28},{12,0},{16,4},{20,8},{24,12},{28,16},{1,21},{... | collective-permute-start | bytes 49160 | tf_op jit(solution)/shard_map/ppermute | solution.py:12
  48.3 6.1 %copy-start.14 = (bf16[512,512]{1,0:T(8,128)(2,1)S(1)}, bf16[512,512]{1,0:T(8,128)(2,1)}, u32[]{:S(2)}) copy-start(bf16[512,512]{1,0:T(8,128)(2,1)} %param.19) | copy-start | bytes 1572868
  62.3 3.9 %copy-start.5 = (f32[384,1024]{1,0:T(8,128)}, f32[384,1024]{1,0:T(8,128)S(1)}, u32[]{:S(2)}) copy-start(f32[384,1024]{1,0:T(8,128)S(1)} %fusion.40) | copy-start | bytes 4718596
  74.0 3.3 %copy-start.3 = (f32[1280,512]{0,1:T(8,128)S(1)}, f32[1280,512]{0,1:T(8,128)}, u32[]{:S(2)}) copy-start(f32[1280,512]{0,1:T(8,128)} %copy-done.2) | copy-start | bytes 7864324
  74.0 4.1 %copy-start.4 = (f32[1280,512]{0,1:T(8,128)S(1)}, f32[1280,512]{0,1:T(8,128)}, u32[]{:S(2)}) copy-start(f32[1280,512]{0,1:T(8,128)} %copy.27) | copy-start | bytes 7864324
  81.2 2.7 copy-start.19
  100.8 4.1 %copy-start.17 = (s32[1280]{0:T(1024)S(1)}, s32[1280]{0:T(1024)}, u32[]{:S(2)}) copy-start(s32[1280]{0:T(1024)} %param.25) | copy-start | bytes 15364
  104.9 21.7 %copy-start.6 = (f32[384,1024]{1,0:T(8,128)S(1)}, f32[384,1024]{1,0:T(8,128)}, u32[]{:S(2)}) copy-start(f32[384,1024]{1,0:T(8,128)} %copy-done.5) | copy-start | bytes 4718596
  107.0 23.7 %collective-permute-start.6 = (bf16[16,512]{1,0:T(8,128)(2,1)S(1)}, bf16[16,512]{1,0:T(8,128)(2,1)S(1)}, u32[]{:S(2)}, u32[]{:S(2)}) collective-permute-start(bf16[16,512]{1,0:T(8,128)(2,1)S(1)} %get-tuple-element.21), channel_id=1, source_target_pairs={{0,28},{4,0},{8,4},{12,8},{16,12},{20,16},{24,20},{28,24},{1,29},{... | collective-permute-start | bytes 49160 | tf_op jit(solution)/shard_map/ppermute | solution.py:12
  112.3 20.7 %collective-permute-start.7 = (bf16[16,512]{1,0:T(8,128)(2,1)S(1)}, bf16[16,512]{1,0:T(8,128)(2,1)S(1)}, u32[]{:S(2)}, u32[]{:S(2)}) collective-permute-start(bf16[16,512]{1,0:T(8,128)(2,1)S(1)} %get-tuple-element.20), channel_id=1, source_target_pairs={{0,4},{4,8},{8,12},{12,16},{16,20},{20,24},{24,28},{28,0},{1,5},{5... | collective-permute-start | bytes 49160 | tf_op jit(solution)/shard_map/ppermute | solution.py:12
  112.3 20.7 %collective-permute-start.8 = (bf16[16,512]{1,0:T(8,128)(2,1)S(1)}, bf16[16,512]{1,0:T(8,128)(2,1)S(1)}, u32[]{:S(2)}, u32[]{:S(2)}) collective-permute-start(bf16[16,512]{1,0:T(8,128)(2,1)S(1)} %get-tuple-element.19), channel_id=1, source_target_pairs={{0,24},{4,28},{8,0},{12,4},{16,8},{20,12},{24,16},{28,20},{1,25},{... | collective-permute-start | bytes 49160 | tf_op jit(solution)/shard_map/ppermute | solution.py:12
  114.1 18.9 %collective-permute-start.9 = (bf16[16,512]{1,0:T(8,128)(2,1)S(1)}, bf16[16,512]{1,0:T(8,128)(2,1)S(1)}, u32[]{:S(2)}, u32[]{:S(2)}) collective-permute-start(bf16[16,512]{1,0:T(8,128)(2,1)S(1)} %get-tuple-element.18), channel_id=1, source_target_pairs={{0,8},{4,12},{8,16},{12,20},{16,24},{20,28},{24,0},{28,4},{1,9},{5... | collective-permute-start | bytes 49160 | tf_op jit(solution)/shard_map/ppermute | solution.py:12
  114.3 18.8 %collective-permute-start.10 = (bf16[16,512]{1,0:T(8,128)(2,1)S(1)}, bf16[16,512]{1,0:T(8,128)(2,1)S(1)}, u32[]{:S(2)}, u32[]{:S(2)}) collective-permute-start(bf16[16,512]{1,0:T(8,128)(2,1)S(1)} %get-tuple-element.17), channel_id=1, source_target_pairs={{0,20},{4,24},{8,28},{12,0},{16,4},{20,8},{24,12},{28,16},{1,21},{... | collective-permute-start | bytes 49160 | tf_op jit(solution)/shard_map/ppermute | solution.py:12
  118.8 11.9 %all-to-all-start.1 = ((bf16[8,2,256]{2,1,0:T(2,128)(2,1)}), bf16[8,2,256]{2,1,0:T(2,128)(2,1)S(1)}, u32[]{:S(2)}, u32[]{:S(2)}) async-start(bf16[8,2,256]{2,1,0:T(2,128)(2,1)} %reshape.250), calls=%async_computation.1 | async-start | bytes 16384 | tf_op jit(solution)/shard_map/all_to_all | solution.py:136
  130.7 6.1 %collective-permute-start.11 = (bf16[16,512]{1,0:T(8,128)(2,1)S(1)}, bf16[16,512]{1,0:T(8,128)(2,1)S(1)}, u32[]{:S(2)}, u32[]{:S(2)}) collective-permute-start(bf16[16,512]{1,0:T(8,128)(2,1)S(1)} %get-tuple-element.16), channel_id=1, source_target_pairs={{0,12},{4,16},{8,20},{12,24},{16,28},{20,0},{24,4},{28,8},{1,13},{... | collective-permute-start | bytes 49160 | tf_op jit(solution)/shard_map/ppermute | solution.py:12
  (19 other events, 29.4 us)
Sparse Core Ops, SparseCore 0:
  99.6 174.7 all-reduce.7
where the time goes:
time: 325 us; the launch traced here: 324 us
  waiting for transfers between devices  141 us (43%)
  local copies, waits for them, and re-layouts  54.6 us (17%)
  starting transfers between devices  36.8 us (11%)
  matrix products  32.1 us (10%)
  blocking collectives  28.5 us (9%)
  other arithmetic  15.3 us (5%)
  between operations  15.2 us (5%)
    unnamed x2, waiting for transfers between devices  135 us
    all_gather x5, blocking collectives, body(): regrouped = lax.all_gather(shares, 'rep', axis=1, tiled=True)  28.5 us
    ppermute x12, starting transfers between devices, passed_along(): return lax.ppermute(x, axis, [(i, (i + by) % peers) for i in range(peers)])  26.6 us
    dot_general x8, matrix products, product_left(): lax.dot_general(left, right, (((0,), (0,)), ((), ())), preferred_element_...  16.2 us
    unnamed x79, local copies, waits for them, and re-layouts  15.6 us
    reshape x5, local copies, waits for them, and re-layouts, body(): gradient.reshape(patches * replicas, -1)  11.8 us
    dot_general x5, matrix products, product(): return jnp.dot(left, right, preferred_element_type=jnp.float32)  8.35 us
    gather x2, local copies, waits for them, and re-layouts, body(): message_grad = input_grad[:, model_width:][edge_receiver] * alive_mask  7.69 us
  transfers between devices with their start and end apart: 15, of which 4 were waited for; matrix products, arithmetic and copies ran while one was open for 8% of the time, Pallas kernels for 0%

commit v1 on v0

v1 whole, which is shorter than its diff:
```python
import functools

import jax
import jax.numpy as jnp
from jax import lax
from jax.experimental import pallas as pl
from jax.experimental.pallas import tpu as pltpu
from jax.sharding import PartitionSpec as P

OCEAN = 32
BANDS = 721
OFFSETS = (1, -1, 2, -2, 3, -3)
MESH = pl.DeviceIdType.MESH
F32 = jnp.float32
BF16 = jnp.bfloat16


def mm(left, right):
    return jnp.dot(left, right, preferred_element_type=F32)


def mm_left(left, right):
    return lax.dot_general(left, right, (((0,), (0,)), ((), ())), preferred_element_type=F32)


def mm_right(left, right):
    return lax.dot_general(left, right, (((1,), (1,)), ((), ())), preferred_element_type=F32)


def logistic(values):
    return 1.0 / (1.0 + jnp.exp(-values))


def mean(values):
    return jnp.mean(values, axis=-1, keepdims=True)


class Stream:
    def __init__(self, refs, sems, split, patch, rep, patches, reps):
        self.own, self.got1, self.acc1, self.got2, self.acc2, self.got3, self.all4, self.fin = refs
        self.send, self.recv = sems
        self.split = split
        self.patch, self.rep, self.patches, self.reps = patch, rep, patches, reps
        self.side = lax.rem(rep, 2)
        self.low, self.high = lax.rem(patch, 2), lax.div(patch, 2)
        self.peer = (patch, rep + 1 - 2 * self.side)
        self.sent = []
        self.wait = []

    def copy(self, src, dst, slot, device):
        c = pltpu.make_async_remote_copy(
            src_ref=src, dst_ref=dst, send_sem=self.send.at[slot], recv_sem=self.recv.at[slot],
            device_id=device, device_id_type=MESH)
        c.start()
        self.sent.append(c)
        self.wait.append(c)

    def arrive(self):
        for c in self.wait:
            c.wait_recv()
        self.wait = []

    def stage1(self):
        src = self.own.at[1 - self.side] if self.split else self.own.at[0]
        self.copy(src, self.got1, 0, self.peer)

    def stage2(self):
        self.arrive()
        mine = self.own[self.side] if self.split else self.own[0]
        self.acc1[...] = (mine.astype(F32) + self.got1[...].astype(F32)).astype(BF16)
        self.copy(self.acc1.at[1 - self.low], self.got2, 1, (self.patch + 1 - 2 * self.low, self.rep))

    def stage3(self):
        self.arrive()
        self.acc2[...] = (self.acc1[self.low].astype(F32) + self.got2[...].astype(F32)).astype(BF16)
        highs = self.patches // 2
        for d in range(1, highs):
            other = lax.rem(self.high + d, highs)
            self.copy(self.acc2.at[other], self.got3.at[d - 1], 1 + d, (2 * other + self.low, self.rep))

    def stage4(self):
        self.arrive()
        highs = self.patches // 2
        total = self.acc2[self.high].astype(F32)
        for d in range(1, highs):
            total = total + self.got3[d - 1].astype(F32)
        rep_highs = self.reps // 2
        here = lax.div(self.rep, 2)
        self.all4[here] = total.astype(BF16)
        for d in range(1, rep_highs):
            other = lax.rem(here + d, rep_highs)
            self.copy(self.all4.at[here], self.all4.at[here], highs + d, (self.patch, 2 * other + self.side))

    def stage5(self, scale):
        self.arrive()
        total = self.all4[0].astype(F32)
        for d in range(1, self.reps // 2):
            total = total + self.all4[d].astype(F32)
        total = total * scale
        if self.split:
            self.fin[self.side] = total
            slot = self.patches // 2 + self.reps // 2
            self.copy(self.fin.at[self.side], self.fin.at[self.side], slot, self.peer)
        else:
            self.fin[0] = total

    def finish(self):
        self.arrive()
        for c in self.sent:
            c.wait_send()


def stream_scratch(rows, width, split, patches, reps):
    highs = patches // 2
    sides = 2 if split else 1
    blocks = (2, highs, rows, width)
    slots = highs + reps // 2 + 1
    return [
        pltpu.VMEM((sides,) + blocks, BF16),
        pltpu.VMEM(blocks, BF16),
        pltpu.VMEM(blocks, BF16),
        pltpu.VMEM(blocks[1:], BF16),
        pltpu.VMEM(blocks[1:], BF16),
        pltpu.VMEM((max(highs - 1, 1), rows, width), BF16),
        pltpu.VMEM((reps // 2, rows, width), BF16),
        pltpu.VMEM((sides, rows, width), F32),
        pltpu.SemaphoreType.DMA((slots,)),
        pltpu.SemaphoreType.DMA((slots,)),
    ]


def put(stream, row, value, patches, split, low=0, rows=None):
    block = value.shape[0] // patches
    rows = block - low if rows is None else rows
    width = value.shape[1] // 2 if split else value.shape[1]
    for p in range(patches):
        for side in range(2 if split else 1):
            stream.own[side, p % 2, p // 2, row : row + rows, :] = value[
                p * block + low : p * block + low + rows, side * width : (side + 1) * width
            ].astype(BF16)


def take(stream, row, rows, out, split):
    if split:
        width = out.shape[1] // 2
        for side in range(2):
            out[:, side * width : (side + 1) * width] = stream.fin[side, row : row + rows, :]
    else:
        out[...] = stream.fin[0, row : row + rows, :]


def kernel(
    dims,
    x, e, tgt, w_ein, w_eout, w_nin, w_nout, w_ro, owners, es, er, count, loss_weight,
    o_node, o_edge, o_ein, o_eout, o_nin, o_nout, o_ro,
    near_out, near_in, far_out, far_in, back_near_out, back_near_in, back_far_out, back_far_in,
    xext, xw, table, sgrad, hid, msg, inv, ezg, epg, agg_grad, total,
    near_send, near_recv, far_send, far_recv, bn_send, bn_recv, bf_send, bf_recv,
    *stream_refs,
):
    patches, reps, slot, far, ext, tile = dims
    nodes, width = x.shape
    edges = e.shape[0]
    near = 6 * slot
    patch, rep = lax.axis_index("patch"), lax.axis_index("rep")
    streams = []
    for i, split in enumerate((True, False, True, True)):
        part = stream_refs[10 * i : 10 * i + 10]
        streams.append(Stream(part[:8], part[8:], split, patch, rep, patches, reps))
    s_node, s_ro, s_one, s_two = streams

    barrier = pltpu.get_barrier_semaphore()
    for d in range(1, patches):
        pl.semaphore_signal(barrier, inc=1, device_id=(lax.rem(patch + d, patches), rep), device_id_type=MESH)
    for d in range(1, reps):
        pl.semaphore_signal(barrier, inc=1, device_id=(patch, lax.rem(rep + d, reps)), device_id_type=MESH)

    own_table = (lax.broadcasted_iota(jnp.int32, (nodes, owners.shape[1]), 0) == owners[...])
    own_table = jnp.where(own_table, 1.0, 0.0).astype(BF16)
    outgoing = mm_left(own_table, x[...])
    for k in range(6):
        near_out[k] = outgoing[k * slot : (k + 1) * slot].astype(BF16)
    for q in range(patches):
        far_out[q] = outgoing[near + q * far : near + (q + 1) * far].astype(BF16)
    pl.semaphore_wait(barrier, patches - 1 + reps - 1)

    def remote(src, dst, send, recv, device):
        c = pltpu.make_async_remote_copy(
            src_ref=src, dst_ref=dst, send_sem=send, recv_sem=recv, device_id=device, device_id_type=MESH)
        c.start()
        return c

    halo = []
    for k, o in enumerate(OFFSETS):
        to = lax.rem(patch + (o + patches), patches)
        halo.append(remote(near_out.at[k], near_in.at[k], near_send.at[k], near_recv.at[k], (to, rep)))
    for d in range(1, patches):
        to = lax.rem(patch + d, patches)
        halo.append(remote(far_out.at[to], far_in.at[patch], far_send.at[d - 1], far_recv.at[d - 1], (to, rep)))
    far_in[patch] = far_out[patch]

    w_s, w_r, w_e = (w_ein.at[pl.ds(i * width, width)] for i in range(3))
    xext[0:nodes, :] = x[...]
    xw[0:nodes, :] = mm(x[...], w_s[...]).astype(BF16)
    xw[ext : ext + nodes, :] = mm(x[...], w_r[...]).astype(BF16)

    def tables(t, _):
        at = pl.ds(pl.multiple_of(t * tile, tile), tile)
        hit = lax.broadcasted_iota(jnp.int32, (ext, tile), 0) == es[:, at]
        table[0:ext, at] = jnp.where(hit, 1.0, 0.0).astype(BF16)
        alive = lax.broadcasted_iota(jnp.int32, (1, tile), 1) + t * tile < count[0]
        ids = jnp.where(alive, er[:, at], -1)
        hit = lax.broadcasted_iota(jnp.int32, (nodes, tile), 0) == ids
        table[ext : ext + nodes, at] = jnp.where(hit, 1.0, 0.0).astype(BF16)
        sgrad[at, :] = mm(e[at, :], w_e[...])
        return 0

    lax.fori_loop(0, edges // tile, tables, 0)

    for c in halo:
        c.wait_recv()
    pieces = [near_in[k] for k in range(6)] + [far_in[q] for q in range(patches)]
    pad = ext - nodes - near - patches * far
    if pad:
        pieces.append(jnp.zeros((pad, width), BF16))
    arrived = jnp.concatenate([v.astype(F32) for v in pieces], axis=0).astype(BF16)
    xext[nodes:ext, :] = arrived
    xw[nodes:ext, :] = mm(arrived, w_s[...]).astype(BF16)

    def edge_forward(t, _):
        at = pl.ds(pl.multiple_of(t * tile, tile), tile)
        pre = sgrad[at, :] + mm_left(table[:, at], xw[...])
        s = logistic(pre)
        hidden = (pre * s).astype(BF16)
        sgrad[at, :] = s * (1.0 + pre * (1.0 - s))
        hid[at, :] = hidden
        z = mm(hidden, w_eout[...])
        centred = z - mean(z)
        inverse = lax.rsqrt(mean(centred * centred) + 1e-05)
        inv[at, :] = inverse
        msg[at, :] = (centred * inverse).astype(BF16)
        return 0

    lax.fori_loop(0, edges // tile, edge_forward, 0)

    aggregate = mm(table[ext : ext + nodes, :], msg[...]).astype(BF16)
    node_pre = mm(x[...], w_nin[0:width, :]) + mm(aggregate, w_nin[width : 2 * width, :])
    s = logistic(node_pre)
    node_hidden = (node_pre * s).astype(BF16)
    node_sgrad = s * (1.0 + node_pre * (1.0 - s))
    z = mm(node_hidden, w_nout[...])
    centred = z - mean(z)
    inverse = lax.rsqrt(mean(centred * centred) + 1e-05)
    normed = centred * inverse
    updated = (x[...].astype(F32) + normed).astype(BF16)
    pred_grad = (loss_weight[...] * (mm(updated, w_ro[...]) - tgt[...].astype(F32))).astype(BF16)
    up_grad = mm_right(pred_grad, w_ro[...])
    z_grad = (inverse * (up_grad - mean(up_grad) - normed * mean(up_grad * normed))).astype(BF16)
    pre_grad = (mm_right(z_grad, w_nout[...]) * node_sgrad).astype(BF16)
    total[...] = up_grad + mm_right(pre_grad, w_nin[0:width, :])
    agg_grad[...] = mm_right(pre_grad, w_nin[width : 2 * width, :]).astype(BF16)
    nin_rows = 2 * width // patches
    put_in = jnp.concatenate([mm_left(x[...], pre_grad), mm_left(aggregate, pre_grad)], axis=0)
    put(s_node, 0, put_in, patches, True)
    put(s_node, nin_rows, mm_left(node_hidden, z_grad), patches, True)
    put(s_ro, 0, mm_left(updated, pred_grad), patches, False)
    s_node.stage1()
    s_ro.stage1()

    def edge_backward(t, _):
        at = pl.ds(pl.multiple_of(t * tile, tile), tile)
        g = mm_left(table[ext : ext + nodes, at], agg_grad[...])
        y = msg[at, :].astype(F32)
        zg = (inv[at, :] * (g - mean(g) - y * mean(g * y))).astype(BF16)
        ezg[at, :] = zg
        epg[at, :] = (mm_right(zg, w_eout[...]) * sgrad[at, :]).astype(BF16)
        return 0

    steps = edges // tile
    first, second = (2 * steps) // 5, (4 * steps) // 5
    lax.fori_loop(0, first, edge_backward, 0)
    s_node.stage2()
    s_ro.stage2()
    lax.fori_loop(first, steps, edge_backward, 0)

    sums32 = mm(table[0:ext, :], epg[...])
    sums = sums32.astype(BF16)
    for k in range(6):
        back_near_out[k] = sums32[nodes + k * slot : nodes + (k + 1) * slot].astype(BF16)
    for q in range(patches):
        at = nodes + near + q * far
        back_far_out[q] = sums32[at : at + far].astype(BF16)
    back = []
    for k, o in enumerate(OFFSETS):
        to = lax.rem(patch + (patches - o), patches)
        back.append(remote(back_near_out.at[k], back_near_in.at[k], bn_send.at[k], bn_recv.at[k], (to, rep)))
    for d in range(1, patches):
        to = lax.rem(patch + d, patches)
        back.append(remote(back_far_out.at[to], back_far_in.at[patch], bf_send.at[d - 1], bf_recv.at[d - 1], (to, rep)))
    back_far_in[patch] = back_far_out[patch]
    share = width // patches
    rsums = mm(table[ext : ext + nodes, :], epg[...]).astype(BF16)
    put_in = jnp.concatenate(
        [mm_left(xext[...], sums), mm_left(x[...], rsums), mm_left(e[...], epg[...])], axis=0)
    put(s_one, 0, put_in, patches, True, 0, share)
    put(s_one, share, mm_left(hid[...], ezg[...]), patches, True)
    s_one.stage1()
    put(s_two, 0, put_in, patches, True, share)
    s_two.stage1()
    s_node.stage3()
    s_ro.stage3()
    s_one.stage2()
    total[...] += mm_right(rsums, w_r[...])

    def edge_out(t, _):
        at = pl.ds(pl.multiple_of(t * tile, tile), tile)
        o_edge[at, :] = mm_right(epg[at, :], w_e[...]).astype(BF16)
        return 0

    s_two.stage2()
    lax.fori_loop(0, first, edge_out, 0)
    s_node.stage4()
    s_ro.stage4()
    lax.fori_loop(first, steps, edge_out, 0)
    for c in back:
        c.wait_recv()
    pieces = [back_near_in[k] for k in range(6)] + [back_far_in[q] for q in range(patches)]
    pad = owners.shape[1] - near - patches * far
    if pad:
        pieces.append(jnp.zeros((pad, width), BF16))
    returned = jnp.concatenate([v.astype(F32) for v in pieces], axis=0).astype(BF16)
    owned = (mm(own_table, returned) + sums32[0:nodes]).astype(BF16)
    o_node[...] = (total[...] + mm_right(owned, w_s[...])).astype(BF16)

    scale = 1.0 / (nodes * patches * reps)
    s_one.stage3()
    s_two.stage3()
    s_node.stage5(scale)
    s_ro.stage5(scale)
    s_one.stage4()
    s_two.stage4()
    s_one.stage5(scale)
    s_two.stage5(scale)
    for c in halo + back:
        c.wait_send()
    s_node.finish()
    s_ro.finish()
    take(s_node, 0, nin_rows, o_nin, True)
    take(s_node, nin_rows, share, o_nout, True)
    take(s_ro, 0, share, o_ro, False)
    s_one.finish()
    take_rows(s_one, 0, share, o_ein, 0)
    take(s_one, share, share, o_eout, True)
    s_two.finish()
    take_rows(s_two, 0, 2 * share, o_ein, share)


def take_rows(stream, row, rows, out, at):
    width = out.shape[1] // 2
    for side in range(2):
        out[at : at + rows, side * width : (side + 1) * width] = stream.fin[side, row : row + rows, :]


def call(
    node_latents, edge_latents, targets, edge_weight_in, edge_weight_out, node_weight_in, node_weight_out,
    readout_weight, send_rows, far_rows, edge_sender, edge_receiver, edge_count, land_mask, lat_band,
):
    nodes, width = node_latents.shape[1:]
    edges = edge_latents.shape[1]
    variables = targets.shape[2]
    patches, reps = lax.axis_size("patch"), lax.axis_size("rep")
    slot = send_rows.shape[1] // 6
    far = far_rows.shape[1] // patches
    near = 6 * slot
    remote_rows = near + patches * far
    ext = -(-(nodes + remote_rows) // 16) * 16
    tile = 256 if edges % 256 == 0 else 128
    listed = -(-remote_rows // 128) * 128
    owners = jnp.concatenate(
        [send_rows[0], far_rows[0], jnp.full((listed - remote_rows,), -1, jnp.int32)])[None]
    latitude = -0.5 * jnp.pi + (lat_band.astype(F32) + 0.5) * (jnp.pi / BANDS)
    channel = lax.iota(jnp.int32, variables)
    keep = jnp.where((channel[None, :] < OCEAN) & (land_mask[:, None] == 1), 0.0, 1.0)
    loss_weight = jnp.cos(latitude)[:, None] * keep
    share = width // patches
    vmem = pl.BlockSpec(memory_space=pltpu.VMEM)
    smem = pl.BlockSpec(memory_space=pltpu.SMEM)
    dma = lambda n: pltpu.SemaphoreType.DMA((n,))
    scratch = [
        pltpu.VMEM((6, slot, width), BF16), pltpu.VMEM((6, slot, width), BF16),
        pltpu.VMEM((patches, far, width), BF16), pltpu.VMEM((patches, far, width), BF16),
        pltpu.VMEM((6, slot, width), BF16), pltpu.VMEM((6, slot, width), BF16),
        pltpu.VMEM((patches, far, width), BF16), pltpu.VMEM((patches, far, width), BF16),
        pltpu.VMEM((ext, width), BF16),
        pltpu.VMEM((ext + nodes, width), BF16),
        pltpu.VMEM((ext + nodes, edges), BF16),
        pltpu.VMEM((edges, width), F32),
        pltpu.VMEM((edges, width), BF16),
        pltpu.VMEM((edges, width), BF16),
        pltpu.VMEM((edges, 1), F32),
        pltpu.VMEM((edges, width), BF16),
        pltpu.VMEM((edges, width), BF16),
        pltpu.VMEM((nodes, width), BF16),
        pltpu.VMEM((nodes, width), F32),
        dma(6), dma(6), dma(patches - 1), dma(patches - 1),
        dma(6), dma(6), dma(patches - 1), dma(patches - 1),
    ]
    scratch += stream_scratch(3 * share, width // 2, True, patches, reps)
    scratch += stream_scratch(share, variables, False, patches, reps)
    scratch += stream_scratch(2 * share, width // 2, True, patches, reps)
    scratch += stream_scratch(2 * share, width // 2, True, patches, reps)
    shape = jax.ShapeDtypeStruct
    outs = pl.pallas_call(
        functools.partial(kernel, (patches, reps, slot, far, ext, tile)),
        out_shape=(
            shape((nodes, width), BF16), shape((edges, width), BF16),
            shape((3 * share, width), F32), shape((share, width), F32),
            shape((2 * share, width), F32), shape((share, width), F32), shape((share, variables), F32),
        ),
        in_specs=[vmem] * 11 + [smem, vmem],
        out_specs=tuple([vmem] * 7),
        scratch_shapes=scratch,
        compiler_params=pltpu.CompilerParams(
            collective_id=0, has_side_effects=True, vmem_limit_bytes=62 * 1024 * 1024),
    )(
        node_latents[0], edge_latents[0], targets[0], edge_weight_in, edge_weight_out, node_weight_in,
        node_weight_out, readout_weight, owners, edge_sender[None], edge_receiver[None], edge_count, loss_weight,
    )
    return (outs[0][None], outs[1][None]) + tuple(outs[2:])


def solution(mesh):
    rows = P("rep", "patch", None)
    in_specs = (rows,) * 3 + (P(),) * 5 + (P("patch", None),) * 2 + (P("patch"),) * 5
    out_specs = (rows,) * 2 + (P("patch", None),) * 5
    return jax.shard_map(call, mesh=mesh, in_specs=in_specs, out_specs=out_specs, check_vma=False)
```

time: 325 us -> 84.6 us (0.26)
  waiting for transfers between devices: 141 us -> 0 us
  Pallas kernels: 0 us -> 69.2 us
  local copies, waits for them, and re-layouts: 54.6 us -> 10.3 us
  starting transfers between devices: 36.8 us -> 0 us
  matrix products: 32.1 us -> 0 us
  blocking collectives: 28.5 us -> 0 us
  between operations: 15.2 us -> 1.3 us
  other arithmetic: 15.3 us -> 3.52 us
    unnamed x2 -> x0, waiting for transfers between devices: 135 us -> none
    pallas_call x0 -> x1, Pallas kernels: none -> 69.2 us  [call(): pl.pallas_call(functools.partial(kernel, (patches, reps, slot, far, ext,...]
    dot_general x19 -> x0, matrix products: 32.1 us -> none  [the longest x8 16.2 us: product_left(): lax.dot_general(left, right, (((0,), (0,)), ((), ())), preferred_element_...]
    all_gather x5 -> x0, blocking collectives: 28.5 us -> none  [body(): regrouped = lax.all_gather(shares, 'rep', axis=1, tiled=True)]
    ppermute x12 -> x0, starting transfers between devices: 26.6 us -> none  [passed_along(): return lax.ppermute(x, axis, [(i, (i + by) % peers) for i in range(peers)])]
    gather x6 -> x0, local copies, waits for them, and re-layouts: 20.6 us -> none  [the longest x2 7.69 us: body(): message_grad = input_grad[:, model_width:][edge_receiver] * alive_mask]
    reshape x9 -> x0, local copies, waits for them, and re-layouts: 14.7 us -> none  [the longest x5 11.8 us: body(): gradient.reshape(patches * replicas, -1)]
    all_to_all x2 -> x0, starting transfers between devices: 10.2 us -> none  [the longest x1 5.1 us: body(): lax.all_to_all(node_rows[far_rows[0]], 'patch', split_axis=0, concat_axis...]
  transfers between devices with their start and end apart: 15 -> 0, of which waited for: 4 -> 0; matrix products, arithmetic and copies ran while one was open for 8% -> 0% of each run, Pallas kernels for 0% -> 0%
where the time goes in v1:
time: 84.6 us; the launch traced here: 84.3 us
  Pallas kernels  69.2 us (82%)
  local copies, waits for them, and re-layouts  10.3 us (12%)
  other arithmetic  3.52 us (4%)
  between operations  1.3 us (2%)
    pallas_call x1, Pallas kernels, call(): pl.pallas_call(functools.partial(kernel, (patches, reps, slot, far, ext,...  69.2 us
    unnamed x17, local copies, waits for them, and re-layouts  7.69 us

profile of v1, /device:TPU:0, one launch (start us, length us, event | category | flops | bytes accessed | tf_op | source)
XLA Modules:
  0.0 84.3 jit_solution(639376619919409167)
XLA Ops:
  1.3 0.7 broadcast_compare_fusion
  2.0 1.3 %add_bitcast_fusion.owners = s32[1,128]{1,0:T(1,128)} fusion(s32[24]{0:T(128)S(1)} %broadcast.11, s32[8]{0:T(128)} %bitcast.14, s32[96]{0:T(128)} %bitcast.15), kind=kLoop, calls=%fused_computation.3 | loop fusion | flops 256 | bytes 1024 | tf_op jit(solution)/shard_map/broadcast_in_dim | solution.py:379
  3.2 0.7 add_cosine_fusion
  4.0 1.3 %broadcast_in_dim.27.es = s32[1,1280]{1,0:T(1,128)} reshape(s32[1280]{0:T(1024)} %param.25) | data formatting | bytes 10240 | tf_op jit(solution)/shard_map/broadcast_in_dim | solution.py:427
  5.3 1.3 %broadcast_in_dim.28.er = s32[1,1280]{1,0:T(1,128)} reshape(s32[1280]{0:T(1024)} %param.26) | data formatting | bytes 10240 | tf_op jit(solution)/shard_map/broadcast_in_dim | solution.py:427
  6.5 0.8 %select_multiply_fusion.loss_weight = f32[384,128]{1,0:T(8,128)} fusion(f32[384]{0:T(512)S(1)} %add_cosine_fusion, pred[128]{0:T(512)(128)(4,1)S(1)} %iota_compare_fusion, pred[384]{0:T(512)(128)(4,1)S(1)} %broadcast_compare_fusion), kind=kLoop, calls=%fused_computation | loop fusion | flops 147456 | bytes 198656 | tf_op jit(solution)/shard_map/mul | solution.py:384
  7.4 69.2 %shard_map.198 = (bf16[384,512]{1,0:T(8,128)(2,1)}, bf16[1280,512]{1,0:T(8,128)(2,1)}, f32[192,512]{1,0:T(8,128)}, f32[64,512]{1,0:T(8,128)}, f32[128,512]{1,0:T...) custom-call(bf16[384,512]{1,0:T(8,128)(2,1)} %bitcast.11, bf16[1280,512]{1,0:T(8,128)(2,1)} %bitcast.10, ...), custom_call_target="tpu_custom_call" | custom-call | tf_op jit(solution)/shard_map/pallas_call | solution.py:413
  76.6 1.8 %copy.30 = bf16[1,384,512]{2,1,0:T(8,128)(2,1)} copy(bf16[1,384,512]{2,1,0:T(8,128)(2,1)} %bitcast.12) | data formatting | bytes 786432
  78.3 0.0 copy-start
  78.4 0.0 copy-start.3
  78.4 0.0 copy-start.1
  78.4 2.5 %copy.31 = bf16[1,1280,512]{2,1,0:T(8,128)(2,1)} copy(bf16[1,1280,512]{2,1,0:T(8,128)(2,1)} %bitcast.9) | data formatting | bytes 2621440
  80.9 0.0 copy-done
  80.9 0.0 copy-start.2
  80.9 0.0 copy-start.4
  80.9 0.7 copy.32
  81.6 0.0 copy-done.3
  81.6 0.7 copy.33
  82.3 0.0 copy-done.1
  82.3 0.7 copy.34
  83.0 0.0 copy-done.2
  83.0 0.7 copy.35
  83.7 0.0 copy-done.4
  83.7 0.6 copy.36
  (2 shorter events, 0.0 us)
Async XLA Ops:
  78.3 2.5 %copy-start = (f32[192,512]{1,0:T(8,128)S(1)}, f32[192,512]{1,0:T(8,128)}, u32[]{:S(2)}) copy-start(f32[192,512]{1,0:T(8,128)} %get-tuple-element.30) | copy-start | bytes 1179652
  78.4 3.3 %copy-start.3 = (f32[64,512]{1,0:T(8,128)S(1)}, f32[64,512]{1,0:T(8,128)}, u32[]{:S(2)}) copy-start(f32[64,512]{1,0:T(8,128)} %get-tuple-element.31) | copy-start | bytes 393220
  78.4 3.9 %copy-start.1 = (f32[128,512]{1,0:T(8,128)S(1)}, f32[128,512]{1,0:T(8,128)}, u32[]{:S(2)}) copy-start(f32[128,512]{1,0:T(8,128)} %get-tuple-element.32) | copy-start | bytes 786436
  80.9 2.1 %copy-start.2 = (f32[64,512]{1,0:T(8,128)S(1)}, f32[64,512]{1,0:T(8,128)}, u32[]{:S(2)}) copy-start(f32[64,512]{1,0:T(8,128)} %get-tuple-element.33) | copy-start | bytes 393220
  80.9 2.8 %copy-start.4 = (f32[64,128]{1,0:T(8,128)S(1)}, f32[64,128]{1,0:T(8,128)}, u32[]{:S(2)}) copy-start(f32[64,128]{1,0:T(8,128)} %get-tuple-element.34) | copy-start | bytes 98308

commit v2 on v1

v2 whole, which is shorter than its diff:
```python
import functools

import jax
import jax.numpy as jnp
from jax import lax
from jax.experimental import pallas as pl
from jax.experimental.pallas import tpu as pltpu
from jax.sharding import PartitionSpec as P

OCEAN = 32
BANDS = 721
OFFSETS = (1, -1, 2, -2, 3, -3)
MESH = pl.DeviceIdType.MESH
F32 = jnp.float32
BF16 = jnp.bfloat16


def mm(left, right):
    return jnp.dot(left, right, preferred_element_type=F32)


def mm_left(left, right):
    return lax.dot_general(left, right, (((0,), (0,)), ((), ())), preferred_element_type=F32)


def mm_right(left, right):
    return lax.dot_general(left, right, (((1,), (1,)), ((), ())), preferred_element_type=F32)


def logistic(values):
    return 1.0 / (1.0 + jnp.exp(-values))


def mean(values):
    return jnp.mean(values, axis=-1, keepdims=True)


class Stream:
    def __init__(self, refs, order, sizes, patch, rep):
        self.order = order
        n = len(order)
        self.own, self.got, self.acc, self.fin = refs[0], refs[1 : 1 + n], refs[1 + n : 1 + 2 * n], refs[1 + 2 * n]
        self.send, self.recv = refs[2 + 2 * n :]
        self.sizes = sizes
        self.patch, self.rep = patch, rep
        self.at = {"side": lax.rem(rep, 2), "wide": lax.div(rep, 2), "low": lax.rem(patch, 2), "high": lax.div(patch, 2)}
        self.reps = sizes["side"] * sizes["wide"]
        self.sent, self.wait, self.slot, self.done = [], [], 0, 0

    def device(self, axis, index):
        at = dict(self.at)
        at[axis] = index
        return (2 * at["high"] + at["low"], 2 * at["wide"] + at["side"])

    def copy(self, src, dst, device):
        c = pltpu.make_async_remote_copy(
            src_ref=src, dst_ref=dst, send_sem=self.send.at[self.slot], recv_sem=self.recv.at[self.slot],
            device_id=device, device_id_type=MESH)
        c.start()
        self.slot += 1
        self.sent.append(c)
        self.wait.append(c)

    def arrive(self):
        for c in self.wait:
            c.wait_recv()
        self.wait = []

    def step(self):
        now, stages = self.done, len(self.order)
        held = self.own
        if now:
            self.arrive()
            axis = self.order[now - 1]
            before = self.own if now == 1 else self.acc[now - 2]
            total = before[self.at[axis]].astype(F32)
            for d in range(1, self.sizes[axis]):
                total = total + self.got[now - 1][d - 1].astype(F32)
            held = self.acc[now - 1]
            held[...] = total.astype(BF16)
        self.done += 1
        if now < stages:
            axis = self.order[now]
            for d in range(1, self.sizes[axis]):
                other = lax.rem(self.at[axis] + d, self.sizes[axis])
                self.copy(held.at[other], self.got[now].at[d - 1], self.device(axis, other))
            return
        mine = self.group(self.rep)
        self.fin[mine] = held[...]
        for other in self.lacking():
            self.copy(held, self.fin.at[mine], (self.patch, other))

    def group(self, rep):
        return rep if "wide" in self.order and "side" in self.order else 0

    def lacking(self):
        return [lax.rem(self.rep + d, self.reps) for d in range(1, self.reps)]

    def finish(self):
        self.arrive()
        for c in self.sent:
            c.wait_send()


class Small(Stream):
    def step(self):
        if self.done < len(self.order):
            return super().step()
        self.arrive()
        axis = self.order[-1]
        total = self.acc[-2][self.at[axis]].astype(F32)
        for d in range(1, self.sizes[axis]):
            total = total + self.got[-1][d - 1].astype(F32)
        self.acc[-1][...] = total.astype(BF16)
        self.fin[self.rep] = self.acc[-1][...]
        for other in self.lacking():
            self.copy(self.acc[-1], self.fin.at[self.rep], (self.patch, other))
        self.done += 1


ORDERS = (
    ("side", "low", "wide", "high"),
    ("side", "wide", "low", "high"),
    ("low", "high"),
    ("side", "low", "wide", "high"),
    ("side", "wide", "low", "high"),
)


def stream_scratch(rows, width, order, sizes):
    lead = tuple(sizes[a] for a in order)
    scratch = [pltpu.VMEM(lead + (rows, width), BF16)]
    slots = sizes["side"] * sizes["wide"] - 1
    for i, axis in enumerate(order):
        scratch.append(pltpu.VMEM((max(sizes[axis] - 1, 1),) + lead[i + 1 :] + (rows, width), BF16))
        slots += sizes[axis] - 1
    for i in range(len(order)):
        scratch.append(pltpu.VMEM(lead[i + 1 :] + (rows, width), BF16))
    scratch.append(pltpu.VMEM((sizes["side"] * sizes["wide"], rows, width), BF16))
    return scratch + [pltpu.SemaphoreType.DMA((slots,)), pltpu.SemaphoreType.DMA((slots,))]


def put(stream, row, value, low=0, rows=None):
    sizes, order = stream.sizes, stream.order
    patches = sizes["low"] * sizes["high"]
    block = value.shape[0] // patches
    rows = block - low if rows is None else rows
    pieces = stream.reps if "side" in order else 1
    width = value.shape[1] // pieces
    for p in range(patches):
        for r in range(pieces):
            at = {"side": r % 2, "wide": r // 2, "low": p % 2, "high": p // 2}
            stream.own[tuple(at[a] for a in order) + (slice(row, row + rows), slice(None))] = value[
                p * block + low : p * block + low + rows, r * width : (r + 1) * width
            ].astype(BF16)


def take(stream, row, rows, out, at, scale):
    if "side" not in stream.order:
        total = stream.fin[0].astype(F32)
        for r in range(1, stream.reps):
            total = total + stream.fin[r].astype(F32)
        out[...] = total * scale
        return
    width = out.shape[1] // stream.reps
    for r in range(stream.reps):
        out[at : at + rows, r * width : (r + 1) * width] = stream.fin[r, row : row + rows, :].astype(F32) * scale


def kernel(
    dims,
    x, e, tgt, w_ein, w_eout, w_nin, w_nout, w_ro, send_ids, far_ids, es, er, count, land, lat,
    o_node, o_edge, o_ein, o_eout, o_nin, o_nout, o_ro,
    near_out, near_in, far_out, far_in, back_near_out, back_near_in, back_far_out, back_far_in,
    xext, xw, table, sgrad, hid, msg, inv, ezg, epg, agg_grad, total,
    near_send, near_recv, far_send, far_recv, bn_send, bn_recv, bf_send, bf_recv,
    *stream_refs,
):
    patches, reps, slot, far, ext, tile = dims
    nodes, width = x.shape
    edges = e.shape[0]
    near = 6 * slot
    patch, rep = lax.axis_index("patch"), lax.axis_index("rep")
    sizes = {"side": 2, "wide": reps // 2, "low": 2, "high": patches // 2}
    streams, used = [], 0
    for order in ORDERS:
        count_refs = 4 + 2 * len(order)
        kind = Stream if "side" in order else Small
        streams.append(kind(stream_refs[used : used + count_refs], order, sizes, patch, rep))
        used += count_refs
    s_in, s_out, s_ro, s_one, s_two = streams

    barrier = pltpu.get_barrier_semaphore()
    for d in range(1, patches):
        pl.semaphore_signal(barrier, inc=1, device_id=(lax.rem(patch + d, patches), rep), device_id_type=MESH)
    for d in range(1, reps):
        pl.semaphore_signal(barrier, inc=1, device_id=(patch, lax.rem(rep + d, reps)), device_id_type=MESH)

    def listed(ids):
        hit = lax.broadcasted_iota(jnp.int32, (nodes, ids.shape[1]), 0) == ids[...]
        return jnp.where(hit, 1.0, 0.0).astype(BF16)

    own_near, own_far = listed(send_ids), listed(far_ids)
    outgoing, outgoing_far = mm_left(own_near, x[...]), mm_left(own_far, x[...])
    for k in range(6):
        near_out[k] = outgoing[k * slot : (k + 1) * slot].astype(BF16)
    for q in range(patches):
        far_out[q] = outgoing_far[q * far : (q + 1) * far].astype(BF16)
    pl.semaphore_wait(barrier, patches - 1 + reps - 1)

    def remote(src, dst, send, recv, device):
        c = pltpu.make_async_remote_copy(
            src_ref=src, dst_ref=dst, send_sem=send, recv_sem=recv, device_id=device, device_id_type=MESH)
        c.start()
        return c

    halo = []
    for k, o in enumerate(OFFSETS):
        to = lax.rem(patch + (o + patches), patches)
        halo.append(remote(near_out.at[k], near_in.at[k], near_send.at[k], near_recv.at[k], (to, rep)))
    for d in range(1, patches):
        to = lax.rem(patch + d, patches)
        halo.append(remote(far_out.at[to], far_in.at[patch], far_send.at[d - 1], far_recv.at[d - 1], (to, rep)))
    far_in[patch] = far_out[patch]

    w_s, w_r, w_e = (w_ein.at[pl.ds(i * width, width)] for i in range(3))
    xext[0:nodes, :] = x[...]
    xw[0:nodes, :] = mm(x[...], w_s[...]).astype(BF16)
    xw[ext : ext + nodes, :] = mm(x[...], w_r[...]).astype(BF16)

    def tables(t, _):
        at = pl.ds(pl.multiple_of(t * tile, tile), tile)
        hit = lax.broadcasted_iota(jnp.int32, (ext, tile), 0) == es[at][None, :]
        table[0:ext, at] = jnp.where(hit, 1.0, 0.0).astype(BF16)
        alive = lax.broadcasted_iota(jnp.int32, (1, tile), 1) + t * tile < count[0]
        ids = jnp.where(alive, er[at][None, :], -1)
        hit = lax.broadcasted_iota(jnp.int32, (nodes, tile), 0) == ids
        table[ext : ext + nodes, at] = jnp.where(hit, 1.0, 0.0).astype(BF16)
        sgrad[at, :] = mm(e[at, :], w_e[...])
        return 0

    lax.fori_loop(0, edges // tile, tables, 0)

    for c in halo:
        c.wait_recv()
    pieces = [near_in[k] for k in range(6)] + [far_in[q] for q in range(patches)]
    pad = ext - nodes - near - patches * far
    if pad:
        pieces.append(jnp.zeros((pad, width), BF16))
    arrived = jnp.concatenate([v.astype(F32) for v in pieces], axis=0).astype(BF16)
    xext[nodes:ext, :] = arrived
    xw[nodes:ext, :] = mm(arrived, w_s[...]).astype(BF16)

    def edge_forward(t, _):
        at = pl.ds(pl.multiple_of(t * tile, tile), tile)
        pre = sgrad[at, :] + mm_left(table[:, at], xw[...])
        s = logistic(pre)
        hidden = (pre * s).astype(BF16)
        sgrad[at, :] = s * (1.0 + pre * (1.0 - s))
        hid[at, :] = hidden
        z = mm(hidden, w_eout[...])
        centred = z - mean(z)
        inverse = lax.rsqrt(mean(centred * centred) + 1e-05)
        inv[at, :] = inverse
        msg[at, :] = (centred * inverse).astype(BF16)
        return 0

    lax.fori_loop(0, edges // tile, edge_forward, 0)

    variables = tgt.shape[1]
    latitude = -0.5 * jnp.pi + (lat[...].astype(F32) + 0.5) * (jnp.pi / BANDS)
    area = jnp.broadcast_to(jnp.cos(latitude)[None, :], (variables, nodes))
    ocean = lax.broadcasted_iota(jnp.int32, (variables, nodes), 0) < OCEAN
    masked = jnp.broadcast_to((land[...])[None, :], (variables, nodes)) == 1
    loss_weight = jnp.transpose(jnp.where(ocean & masked, 0.0, area))
    aggregate = mm(table[ext : ext + nodes, :], msg[...]).astype(BF16)
    node_pre = mm(x[...], w_nin[0:width, :]) + mm(aggregate, w_nin[width : 2 * width, :])
    s = logistic(node_pre)
    node_hidden = (node_pre * s).astype(BF16)
    node_sgrad = s * (1.0 + node_pre * (1.0 - s))
    z = mm(node_hidden, w_nout[...])
    centred = z - mean(z)
    inverse = lax.rsqrt(mean(centred * centred) + 1e-05)
    normed = centred * inverse
    updated = (x[...].astype(F32) + normed).astype(BF16)
    pred_grad = (loss_weight * (mm(updated, w_ro[...]) - tgt[...].astype(F32))).astype(BF16)
    up_grad = mm_right(pred_grad, w_ro[...])
    z_grad = (inverse * (up_grad - mean(up_grad) - normed * mean(up_grad * normed))).astype(BF16)
    pre_grad = (mm_right(z_grad, w_nout[...]) * node_sgrad).astype(BF16)
    total[...] = up_grad + mm_right(pre_grad, w_nin[0:width, :])
    agg_grad[...] = mm_right(pre_grad, w_nin[width : 2 * width, :]).astype(BF16)
    share = width // patches
    put(s_in, 0, jnp.concatenate([mm_left(x[...], pre_grad), mm_left(aggregate, pre_grad)], axis=0))
    s_in.step()
    put(s_out, 0, mm_left(node_hidden, z_grad))
    s_out.step()
    put(s_ro, 0, mm_left(updated, pred_grad))
    s_ro.step()

    def edge_backward(t, _):
        at = pl.ds(pl.multiple_of(t * tile, tile), tile)
        g = mm_left(table[ext : ext + nodes, at], agg_grad[...])
        y = msg[at, :].astype(F32)
        zg = (inv[at, :] * (g - mean(g) - y * mean(g * y))).astype(BF16)
        ezg[at, :] = zg
        epg[at, :] = (mm_right(zg, w_eout[...]) * sgrad[at, :]).astype(BF16)
        return 0

    steps = edges // tile
    cuts = [0, steps // 5, (2 * steps) // 5, (3 * steps) // 5, steps]
    lax.fori_loop(cuts[0], cuts[1], edge_backward, 0)
    s_in.step()
    s_out.step()
    lax.fori_loop(cuts[1], cuts[3], edge_backward, 0)
    s_out.step()
    s_in.step()
    lax.fori_loop(cuts[3], cuts[4], edge_backward, 0)
    s_ro.step()
    s_out.step()
    s_in.step()

    sums32 = mm(table[0:ext, :], epg[...])
    sums = sums32.astype(BF16)
    for k in range(6):
        back_near_out[k] = sums32[nodes + k * slot : nodes + (k + 1) * slot].astype(BF16)
    for q in range(patches):
        at = nodes + near + q * far
        back_far_out[q] = sums32[at : at + far].astype(BF16)
    back = []
    for k, o in enumerate(OFFSETS):
        to = lax.rem(patch + (patches - o), patches)
        back.append(remote(back_near_out.at[k], back_near_in.at[k], bn_send.at[k], bn_recv.at[k], (to, rep)))
    for d in range(1, patches):
        to = lax.rem(patch + d, patches)
        back.append(remote(back_far_out.at[to], back_far_in.at[patch], bf_send.at[d - 1], bf_recv.at[d - 1], (to, rep)))
    back_far_in[patch] = back_far_out[patch]
    rsums = mm(table[ext : ext + nodes, :], epg[...]).astype(BF16)
    put_in = jnp.concatenate(
        [mm_left(xext[...], sums), mm_left(x[...], rsums), mm_left(e[...], epg[...])], axis=0)
    put(s_two, 0, put_in, share)
    s_two.step()
    put(s_one, 0, put_in, 0, share)
    put(s_one, share, mm_left(hid[...], ezg[...]))
    s_one.step()
    s_two.step()
    s_one.step()
    total[...] += mm_right(rsums, w_r[...])

    def edge_out(t, _):
        at = pl.ds(pl.multiple_of(t * tile, tile), tile)
        o_edge[at, :] = mm_right(epg[at, :], w_e[...]).astype(BF16)
        return 0

    lax.fori_loop(0, steps, edge_out, 0)
    s_ro.step()
    s_in.step()
    s_out.step()
    for c in back:
        c.wait_recv()
    near_back = jnp.concatenate([back_near_in[k] for k in range(6)], axis=0)
    far_back = jnp.concatenate([back_far_in[q].astype(F32) for q in range(patches)], axis=0).astype(BF16)
    owned = mm(own_near, near_back) + mm(own_far, far_back)
    owned = (owned + sums32[0:nodes]).astype(BF16)
    o_node[...] = (total[...] + mm_right(owned, w_s[...])).astype(BF16)

    scale = 1.0 / (nodes * patches * reps)
    for _ in range(3):
        s_two.step()
        s_one.step()
    for c in halo + back:
        c.wait_send()
    s_in.finish()
    s_out.finish()
    s_ro.finish()
    take(s_in, 0, 2 * share, o_nin, 0, scale)
    take(s_out, 0, share, o_nout, 0, scale)
    take(s_ro, 0, share, o_ro, 0, scale)
    s_one.finish()
    take(s_one, 0, share, o_ein, 0, scale)
    take(s_one, share, share, o_eout, 0, scale)
    s_two.finish()
    take(s_two, 0, 2 * share, o_ein, share, scale)


def settle_kernel(n, *refs):
    src, dst, held = refs[:n], refs[n : 2 * n], refs[2 * n : 3 * n]
    sem_in, sem_out = refs[3 * n :]
    into = [pltpu.make_async_copy(src[i], held[i], sem_in.at[i]) for i in range(n)]
    out = [pltpu.make_async_copy(held[i], dst[i], sem_out.at[i]) for i in range(n)]
    for c in into:
        c.start()
    for i in range(n):
        into[i].wait()
        out[i].start()
    for c in out:
        c.wait()


def settle(arrays):
    n = len(arrays)
    hbm = pl.BlockSpec(memory_space=pl.ANY)
    return pl.pallas_call(
        functools.partial(settle_kernel, n),
        out_shape=tuple(jax.ShapeDtypeStruct(a.shape, a.dtype) for a in arrays),
        in_specs=[hbm] * n,
        out_specs=tuple([hbm] * n),
        scratch_shapes=[pltpu.VMEM(a.shape, a.dtype) for a in arrays]
        + [pltpu.SemaphoreType.DMA((n,)), pltpu.SemaphoreType.DMA((n,))],
    )(*arrays)


def call(
    node_latents, edge_latents, targets, edge_weight_in, edge_weight_out, node_weight_in, node_weight_out,
    readout_weight, send_rows, far_rows, edge_sender, edge_receiver, edge_count, land_mask, lat_band,
):
    nodes, width = node_latents.shape[1:]
    edges = edge_latents.shape[1]
    variables = targets.shape[2]
    patches, reps = lax.axis_size("patch"), lax.axis_size("rep")
    slot = send_rows.shape[1] // 6
    far = far_rows.shape[1] // patches
    near = 6 * slot
    remote_rows = near + patches * far
    ext = -(-(nodes + remote_rows) // 16) * 16
    tile = 256 if edges % 256 == 0 else 128
    share = width // patches
    vmem = pl.BlockSpec(memory_space=pltpu.VMEM)
    smem = pl.BlockSpec(memory_space=pltpu.SMEM)
    dma = lambda n: pltpu.SemaphoreType.DMA((n,))
    scratch = [
        pltpu.VMEM((6, slot, width), BF16), pltpu.VMEM((6, slot, width), BF16),
        pltpu.VMEM((patches, far, width), BF16), pltpu.VMEM((patches, far, width), BF16),
        pltpu.VMEM((6, slot, width), BF16), pltpu.VMEM((6, slot, width), BF16),
        pltpu.VMEM((patches, far, width), BF16), pltpu.VMEM((patches, far, width), BF16),
        pltpu.VMEM((ext, width), BF16),
        pltpu.VMEM((ext + nodes, width), BF16),
        pltpu.VMEM((ext + nodes, edges), BF16),
        pltpu.VMEM((edges, width), F32),
        pltpu.VMEM((edges, width), BF16),
        pltpu.VMEM((edges, width), BF16),
        pltpu.VMEM((edges, 1), F32),
        pltpu.VMEM((edges, width), BF16),
        pltpu.VMEM((edges, width), BF16),
        pltpu.VMEM((nodes, width), BF16),
        pltpu.VMEM((nodes, width), F32),
        dma(6), dma(6), dma(patches - 1), dma(patches - 1),
        dma(6), dma(6), dma(patches - 1), dma(patches - 1),
    ]
    sizes = {"side": 2, "wide": reps // 2, "low": 2, "high": patches // 2}
    for order, count in zip(ORDERS, (2 * share, share, share, 2 * share, 2 * share)):
        scratch += stream_scratch(count, width // reps if "side" in order else variables, order, sizes)
    shape = jax.ShapeDtypeStruct
    outs = pl.pallas_call(
        functools.partial(kernel, (patches, reps, slot, far, ext, tile)),
        out_shape=(
            shape((nodes, width), BF16), shape((edges, width), BF16),
            shape((3 * share, width), F32), shape((share, width), F32),
            shape((2 * share, width), F32), shape((share, width), F32), shape((share, variables), F32),
        ),
        in_specs=[vmem] * 12 + [smem] + [vmem] * 2,
        out_specs=tuple([vmem] * 7),
        scratch_shapes=scratch,
        compiler_params=pltpu.CompilerParams(
            collective_id=0, has_side_effects=True, vmem_limit_bytes=62 * 1024 * 1024),
    )(
        node_latents[0], edge_latents[0], targets[0], edge_weight_in, edge_weight_out, node_weight_in,
        node_weight_out, readout_weight, send_rows, far_rows, edge_sender, edge_receiver, edge_count,
        land_mask, lat_band,
    )
    outs = settle(outs)
    return (outs[0][None], outs[1][None]) + tuple(outs[2:])


def solution(mesh):
    rows = P("rep", "patch", None)
    in_specs = (rows,) * 3 + (P(),) * 5 + (P("patch", None),) * 2 + (P("patch"),) * 5
    out_specs = (rows,) * 2 + (P("patch", None),) * 5
    return jax.shard_map(call, mesh=mesh, in_specs=in_specs, out_specs=out_specs, check_vma=False)
```

time: 84.6 us -> 71 us (0.84)
  local copies, waits for them, and re-layouts: 10.3 us -> 0 us
  other arithmetic: 3.52 us -> 0 us
    unnamed x17 -> x0, local copies, waits for them, and re-layouts: 7.69 us -> none
    pallas_call x0 -> x1, Pallas kernels: none -> 2.92 us  [settle(): pl.pallas_call(functools.partial(settle_kernel, n), out_shape=tuple((jax....]
    broadcast_in_dim x2 -> x0, local copies, waits for them, and re-layouts: 2.59 us -> none  [the longest x1 1.3 us: call(): edge_sender[None]]
    pallas_call x1, Pallas kernels: 69.2 us -> 66.6 us  [call(): pl.pallas_call(functools.partial(kernel, (patches, reps, slot, far, ext,...]
    broadcast_in_dim x1 -> x0, other arithmetic: 1.26 us -> none  [call(): jnp.concatenate([send_rows[0], far_rows[0], jnp.full((listed - remote_row...]
where the time goes in v2:
time: 71 us; the launch traced here: 70.8 us
  Pallas kernels  69.5 us (98%)
  between operations  1.29 us (2%)
    pallas_call x1, Pallas kernels, call(): pl.pallas_call(functools.partial(kernel, (patches, reps, slot, far, ext,...  66.6 us
    pallas_call x1, Pallas kernels, settle(): pl.pallas_call(functools.partial(settle_kernel, n), out_shape=tuple((jax....  2.92 us

profile of v2, /device:TPU:0, one launch (start us, length us, event | category | flops | bytes accessed | tf_op | source)
XLA Modules:
  0.0 70.8 jit_solution(17816542430831299407)
XLA Ops:
  1.3 66.6 %shard_map.198 = (bf16[384,512]{1,0:T(8,128)(2,1)}, bf16[1280,512]{1,0:T(8,128)(2,1)}, f32[192,512]{1,0:T(8,128)}, f32[64,512]{1,0:T(8,128)}, f32[128,512]{1,0:T...) custom-call(bf16[384,512]{1,0:T(8,128)(2,1)} %bitcast.6, bf16[1280,512]{1,0:T(8,128)(2,1)} %bitcast.5, ...), custom_call_target="tpu_custom_call" | custom-call | tf_op jit(solution)/shard_map/pallas_call | solution.py:453
  67.9 2.9 %shard_map.199 = (bf16[384,512]{1,0:T(8,128)(2,1)}, bf16[1280,512]{1,0:T(8,128)(2,1)}, f32[192,512]{1,0:T(8,128)}, f32[64,512]{1,0:T(8,128)}, f32[128,512]{1,0:T...) custom-call(bf16[384,512]{1,0:T(8,128)(2,1)} %get-tuple-element.21.refs_0_, bf16[1280,512]{1,0:T(8,128)(2,1)} %get-tuple-element.22.refs_1_, ...), custom_call_target="tpu_custom_call" | custom-call | tf_op jit(solution)/shard_map/pallas_call | solution.py:402

commit v3 on v2

--- a/solution.py
+++ b/solution.py
@@ -311,13 +311,10 @@
     lax.fori_loop(cuts[0], cuts[1], edge_backward, 0)
     s_in.step()
     s_out.step()
-    lax.fori_loop(cuts[1], cuts[3], edge_backward, 0)
+    lax.fori_loop(cuts[1], cuts[4], edge_backward, 0)
     s_out.step()
     s_in.step()
-    lax.fori_loop(cuts[3], cuts[4], edge_backward, 0)
     s_ro.step()
-    s_out.step()
-    s_in.step()
 
     sums32 = mm(table[0:ext, :], epg[...])
     sums = sums32.astype(BF16)
@@ -344,6 +341,8 @@
     s_one.step()
     s_two.step()
     s_one.step()
+    s_out.step()
+    s_in.step()
     total[...] += mm_right(rsums, w_r[...])
 
     def edge_out(t, _):

time: 71 us -> 64.6 us (0.910)
  Pallas kernels: 69.5 us -> 63.2 us
    pallas_call x1, Pallas kernels: 66.6 us -> 60.2 us  [call(): pl.pallas_call(functools.partial(kernel, (patches, reps, slot, far, ext,...]
where the time goes in v3:
time: 64.6 us; the launch traced here: 64.4 us
  Pallas kernels  63.2 us (98%)
  between operations  1.29 us (2%)
    pallas_call x1, Pallas kernels, call(): pl.pallas_call(functools.partial(kernel, (patches, reps, slot, far, ext,...  60.2 us
    pallas_call x1, Pallas kernels, settle(): pl.pallas_call(functools.partial(settle_kernel, n), out_shape=tuple((jax....  2.92 us

profile of v3, /device:TPU:0, one launch (start us, length us, event | category | flops | bytes accessed | tf_op | source)
XLA Modules:
  0.0 64.4 jit_solution(5897662829371646562)
XLA Ops:
  1.3 60.2 %shard_map.198 = (bf16[384,512]{1,0:T(8,128)(2,1)}, bf16[1280,512]{1,0:T(8,128)(2,1)}, f32[192,512]{1,0:T(8,128)}, f32[64,512]{1,0:T(8,128)}, f32[128,512]{1,0:T...) custom-call(bf16[384,512]{1,0:T(8,128)(2,1)} %bitcast.6, bf16[1280,512]{1,0:T(8,128)(2,1)} %bitcast.5, ...), custom_call_target="tpu_custom_call" | custom-call | tf_op jit(solution)/shard_map/pallas_call | solution.py:452
  61.5 2.9 %shard_map.199 = (bf16[384,512]{1,0:T(8,128)(2,1)}, bf16[1280,512]{1,0:T(8,128)(2,1)}, f32[192,512]{1,0:T(8,128)}, f32[64,512]{1,0:T(8,128)}, f32[128,512]{1,0:T...) custom-call(bf16[384,512]{1,0:T(8,128)(2,1)} %get-tuple-element.21.refs_0_, bf16[1280,512]{1,0:T(8,128)(2,1)} %get-tuple-element.22.refs_1_, ...), custom_call_target="tpu_custom_call" | custom-call | tf_op jit(solution)/shard_map/pallas_call | solution.py:401
